TPU v7x, 32 devices: a whole 2x2x4 slice. The times are simulated.
32 devices in a mesh: row: 4 (over z), col: 8 (over y, x, core).
Axes of the slice: x: 2, y: 2, z: 4, core: 2. Of those that a mesh axis runs over, the one named last changes fastest.
Arguments:
- clean: float32 [1344, 8192], P('row', 'col'), may hold values from -6 to 6
- noise: float32 [1344, 8192], P('row', 'col'), may hold values from -6 to 6
- bucket: int32 [32], replicated, may hold values from 0 to 31
- mod_table: float32 [1, 32, 1344], replicated, may hold values from -3 to 3
- w_first: float32 [1, 1344, 1344], P(None, 'row', 'col'), may hold values from -0.15625 to 0.15625
- w_second: float32 [1, 1344, 1344], P(None, 'col', 'row'), may hold values from -0.15625 to 0.15625
Outputs:
- grad_first: float32 [1, 1344, 1344], P(None, 'row', 'col')
- grad_second: float32 [1, 1344, 1344], P(None, 'col', 'row')
All inputs are finite; a program needn't handle non-finite values.
Results may differ from a plain program's by a relative error of at most 0.018.
Values may be sent and summed in bfloat16 or wider, within the bound.
A program may use at most 64 MiB of HBM per device.

v0:
```python
import math

import jax
import jax.numpy as jnp
from jax import lax
from jax.sharding import PartitionSpec as P

PIX = 256
BUCKETS = 32


MIX_WEIGHT = 0.3
KEEP_COEF = (1.0 - MIX_WEIGHT) / math.sqrt((1.0 - MIX_WEIGHT) ** 2 + MIX_WEIGHT**2)
ADD_COEF = MIX_WEIGHT / math.sqrt((1.0 - MIX_WEIGHT) ** 2 + MIX_WEIGHT**2)
SILU_GAIN = 1.0 / 0.596
CONTRACT_LEAD = (((0,), (0,)), ((), ()))
CONTRACT_TAIL = (((1,), (1,)), ((), ()))


def noise_levels(bucket):
    return jnp.exp(-3.0 + 5.0 * (bucket.astype(jnp.float32) + 0.5) / BUCKETS)


def silu_slope(values):
    sig = jax.nn.sigmoid(values)
    return sig * (1.0 + values * (1.0 - sig))


def bucket_gains(table, picked):
    onehot = (picked[:, None] == jnp.arange(table.shape[0], dtype=jnp.int32)[None, :]).astype(
        jnp.float32
    )
    return jnp.dot(
        onehot, table, precision=lax.Precision.HIGHEST, preferred_element_type=jnp.float32
    )


def local(clean, noise, bucket, mod_table, w_first, w_second):
    rows_size = lax.axis_size("row")
    row_at = lax.axis_index("row")
    col_at = lax.axis_index("col")
    samples = bucket.shape[0]
    own_rows = clean.shape[1]
    weight_first = w_first[0]
    weight_second = w_second[0]
    table = 1.0 + mod_table[0]
    col_first = jnp.sqrt(lax.psum(jnp.sum(weight_first * weight_first, axis=0), "row") + 1.0)
    col_second = jnp.sqrt(lax.psum(jnp.sum(weight_second * weight_second, axis=0), "col") + 1.0)
    normed_first = (weight_first / col_first[None, :]).astype(jnp.bfloat16)
    normed_second = (weight_second / col_second[None, :]).astype(jnp.bfloat16)
    chan_clean, chan_noise = (
        lax.all_to_all(
            clean.astype(jnp.bfloat16), "row", split_axis=1, concat_axis=0, tiled=True
        ).astype(clean.dtype),
        lax.all_to_all(
            noise.astype(jnp.bfloat16), "row", split_axis=1, concat_axis=0, tiled=True
        ).astype(noise.dtype),
    )
    local_clean = chan_clean.T
    local_noise = chan_noise.T
    sub_rows = own_rows // rows_size
    first_row = col_at * own_rows + row_at * sub_rows
    row_sample = (first_row + jnp.arange(sub_rows, dtype=jnp.int32)) // PIX
    row_bucket = jnp.take(bucket, row_sample)
    levels = noise_levels(row_bucket)[:, None]
    spread_root = jnp.sqrt(levels * levels + 0.25)
    state_own = ((local_clean + levels * local_noise) / spread_root).astype(jnp.bfloat16)
    target = local_clean * (2.0 * levels / spread_root) - local_noise * (0.5 / spread_root)
    gains = bucket_gains(table, row_bucket)
    part_first, part_second = (
        lax.all_gather(normed_first, "col", axis=1, tiled=True),
        lax.all_gather(normed_second, "col", axis=0, tiled=True),
    )
    full_first, full_second = (
        lax.all_gather(part_first, "row", axis=0, tiled=True),
        lax.all_gather(part_second, "row", axis=1, tiled=True),
    )
    pre_act = jnp.dot(state_own, full_first, preferred_element_type=jnp.float32)
    hidden = (jax.nn.silu(pre_act) * SILU_GAIN * gains).astype(jnp.bfloat16)
    branch = jnp.dot(hidden, full_second, preferred_element_type=jnp.float32)
    state_new = (KEEP_COEF * state_own.astype(jnp.float32) + ADD_COEF * branch).astype(jnp.bfloat16)
    grad_own = (state_new.astype(jnp.float32) - target) / samples
    dbranch = (ADD_COEF * grad_own).astype(jnp.bfloat16)
    gsecond_full = lax.dot_general(
        hidden, dbranch, CONTRACT_LEAD, preferred_element_type=jnp.float32
    )
    dhidden = lax.dot_general(
        dbranch, full_second, CONTRACT_TAIL, preferred_element_type=jnp.float32
    )
    dpre = (dhidden * gains * silu_slope(pre_act) * SILU_GAIN).astype(jnp.bfloat16)
    gfirst_full = lax.dot_general(
        state_own, dpre, CONTRACT_LEAD, preferred_element_type=jnp.float32
    )
    part_gfirst, part_gsecond = (
        lax.psum_scatter(
            gfirst_full.astype(jnp.bfloat16), "col", scatter_dimension=1, tiled=True
        ).astype(jnp.float32),
        lax.psum_scatter(
            gsecond_full.astype(jnp.bfloat16), "col", scatter_dimension=0, tiled=True
        ).astype(jnp.float32),
    )
    gfirst, gsecond = (
        lax.psum_scatter(
            part_gfirst.astype(jnp.bfloat16), "row", scatter_dimension=0, tiled=True
        ).astype(jnp.float32),
        lax.psum_scatter(
            part_gsecond.astype(jnp.bfloat16), "row", scatter_dimension=1, tiled=True
        ).astype(jnp.float32),
    )
    dot_first = lax.psum(jnp.sum(weight_first * gfirst, axis=0), "row")
    dot_second = lax.psum(jnp.sum(weight_second * gsecond, axis=0), "col")
    grad_first = gfirst / col_first[None, :] - weight_first * (dot_first / col_first**3)[None, :]
    grad_second = (
        gsecond / col_second[None, :] - weight_second * (dot_second / col_second**3)[None, :]
    )
    return (grad_first[None], grad_second[None])


def solution(mesh):
    placed = (
        P("row", "col"),
        P("row", "col"),
        P(),
        P(),
        P(None, "row", "col"),
        P(None, "col", "row"),
    )
    return jax.shard_map(
        local,
        mesh=mesh,
        in_specs=placed,
        out_specs=(P(None, "row", "col"), P(None, "col", "row")),
        check_vma=False,
    )
```

profile of v0, /device:TPU:0, one launch (start us, length us, event | category | flops | bytes accessed | tf_op | source)
XLA Modules:
  0.0 391.9 jit_solution(4668618831318056864)
XLA Ops:
  7.2 1.1 fusion.23
  8.3 13.5 %psum.28 = f32[168]{0:T(256)S(1)} all-reduce(f32[168]{0:T(256)S(1)} %fusion.23), channel_id=1, replica_groups=mesh['row'=4,'col'=8] {'row'}, use_global_device_ids=true, to_apply=%region_1.0 | all-reduce | flops 168 | bytes 1344 | tf_op jit(solution)/shard_map/psum | solution.py:47
  21.8 1.0 fusion.24
  22.8 11.0 %all_gather.12 = bf16[336,1344]{0,1:T(8,128)(2,1)S(1)} all-gather(bf16[336,168]{0,1:T(8,128)(2,1)S(1)} %fusion.24), channel_id=1, replica_groups=mesh['row'=4,'col'=8] {'col'}, dimensions={1}, use_global_device_ids=true | all-gather | bytes 1016064 | tf_op jit(solution)/shard_map/all_gather | solution.py:71
  33.8 1.8 copy.22
  35.7 13.3 %psum.29 = f32[336]{0:T(512)S(1)} all-reduce(f32[336]{0:T(512)S(1)} %fusion.21), channel_id=1, replica_groups=mesh['row'=4,'col'=8] {'col'}, use_global_device_ids=true, to_apply=%region_3.0 | all-reduce | flops 336 | bytes 2688 | tf_op jit(solution)/shard_map/psum | solution.py:48
  49.0 11.3 %all_gather.14 = bf16[1344,336]{1,0:T(8,128)(2,1)S(1)} all-gather(bf16[168,336]{1,0:T(8,128)(2,1)S(1)} %fusion.22), channel_id=1, replica_groups=mesh['row'=4,'col'=8] {'col'}, dimensions={0}, use_global_device_ids=true | all-gather | bytes 1016064 | tf_op jit(solution)/shard_map/all_gather | solution.py:72
  60.3 1.8 copy.23
  63.2 3.5 all-to-all-start
  67.7 38.2 %all-to-all-done = bf16[336,4,256]{2,0,1:T(8,128)(2,1)S(1)} async-done(((bf16[336,4,256]{2,0,1:T(8,128)(2,1)}), bf16[336,4,256]{2,0,1:T(8,128)(2,1)S(1)}, u32[]{:S(2)}, u32[]{:S(2)}) %all-to-all-start) | async-done | bytes 688160 | tf_op jit(solution)/shard_map/all_to_all | solution.py:52
  105.9 3.5 all-to-all-start.1
  110.8 4.3 %compare_select_fusion.1 = s32[256,1]{0,1:T(1,128)S(1)} fusion(s32[]{:T(128)} %bitcast.27, s32[]{:T(128)} %bitcast.28, s32[]{:T(128)} %bitcast.29, s32[]{:T(128)} %bitcast.30, s32[]{:T(128)} %bitcast.31, s32[]{:T(128)} %bitcast.33, s32[]{:T(128)} %bitcast.32, s32[]{:T(128)S(6)} %add.205), kind=kLoop, calls=%fused_computation.78 | loop fusion | flops 7936 | bytes 1056 | tf_op jit(solution)/shard_map/jit(_take)/gather | solution.py:64
  115.8 15.7 %multiply_multiply_fusion.2 = (f32[256]{0:T(256)S(1)}, s32[256]{0:T(256)S(1)}) fusion(pred[256]{0:T(512)(128)(4,1)S(1)} %get-tuple-element.45, pred[256]{0:T(512)(128)(4,1)S(1)} %get-tuple-element.46, pred[256]{0:T(512)(128)(4,1)S(1)} %get-tuple-element.47, pred[256]{0:T(512)(128)(4,1)S(1)} %get-tuple-element.48, pred[256]{0:T(512)(128)(4,1)S(1)} %get-tuple-element.49, ...), kind=kLoop, calls=%fused_computation.99 | loop fusion | flops 14336 | bytes 9576 | tf_op jit(solution)/shard_map/div | solution.py:68
  131.5 4.5 %all-to-all-done.1 = bf16[336,4,256]{2,0,1:T(8,128)(2,1)S(1)} async-done(((bf16[336,4,256]{2,0,1:T(8,128)(2,1)}), bf16[336,4,256]{2,0,1:T(8,128)(2,1)S(1)}, u32[]{:S(2)}, u32[]{:S(2)}) %all-to-all-start.1) | async-done | bytes 688160 | tf_op jit(solution)/shard_map/all_to_all | solution.py:55
  136.0 1.3 fusion.12
  137.3 4.0 %fusion.38 = f32[256,1344]{0,1:T(8,128)S(1)} fusion(bf16[1344,256]{1,0:T(8,128)(2,1)} %get-tuple-element.7, bf16[1344,1344]{1,0:T(8,128)(2,1)} %all-gather.3.cloned.1.call-done), kind=kOutput, calls=%fused_computation.110 | convolution fusion | flops 924844032 | bytes 5677056 | tf_op jit(solution)/shard_map/dot_general | solution.py:78
  141.3 1.1 copy-done.8
  142.4 2.1 multiply_convert_fusion
  144.5 65.3 %all-gather.5.cloned.1.call-done = bf16[1344,1344]{0,1:T(8,128)(2,1)} async-done(((bf16[1344,336]{0,1:T(8,128)(2,1)}), bf16[1344,1344]{0,1:T(8,128)(2,1)}) %all-gather.5.cloned.1.call-update) | async-done | bytes 3612688 | tf_op jit(solution)/shard_map/all_gather | solution.py:76
  209.8 4.3 %fusion.8 = bf16[256,1344]{0,1:T(8,128)(2,1)} fusion(bf16[1344,1344]{0,1:T(8,128)(2,1)} %all-gather.5.cloned.1.call-done, bf16[256,1344]{0,1:T(8,128)(2,1)S(1)} %get-tuple-element.43, f32[1344,256]{1,0:T(8,128)S(1)} %get-tuple-element.6, bf16[1344,256]{1,0:T(8,128)(2,1)S(1)} %copy-done.4), kind=kOutput, calls=%fused_computation.12 | convolution fusion | flops 927940608 | bytes 7053312 | tf_op jit(solution)/shard_map/dot_general | solution.py:80
  214.1 9.4 %convolution_convert_fusion.1 = bf16[1344,1344]{0,1:T(8,128)(2,1)} fusion(bf16[1344,256]{1,0:T(8,128)(2,1)S(1)} %copy-done.4, f32[256,1344]{0,1:T(8,128)} %get-tuple-element.44, bf16[256,1344]{0,1:T(8,128)(2,1)} %fusion.8, bf16[1344,1344]{0,1:T(8,128)(2,1)} %all-gather.5.cloned.1.call-done, f32[256,1344]{0,1:T(8,128)} %copy-done.8), kind=kOutput, calls=%fused_computation.1 | convolution fusion | flops 1855279104 | bytes 11354112 | tf_op jit(solution)/shard_map/dot_general | solution.py:91
  224.6 3.2 convolution_convert_fusion
  227.9 42.8 %reduce-scatter.17.cloned.1.call-done = bf16[1344,168]{0,1:T(8,128)(2,1)} async-done(((bf16[1344,1344]{0,1:T(8,128)(2,1)}), bf16[1344,168]{0,1:T(8,128)(2,1)}) %reduce-scatter.17.cloned.1.call-update) | async-done | bytes 451600
  270.7 2.1 copy.24
  272.9 49.7 %reduce-scatter.19.cloned.1.call-done = bf16[168,1344]{1,0:T(8,128)(2,1)} async-done(((bf16[1344,1344]{1,0:T(8,128)(2,1)}), bf16[168,1344]{1,0:T(8,128)(2,1)}) %reduce-scatter.19.cloned.1.call-update) | async-done | bytes 451600
  322.7 2.2 copy.26
  324.9 22.8 %reduce-scatter.13.cloned.1.call-done = bf16[336,168]{1,0:T(8,128)(2,1)} async-done(((bf16[1344,168]{1,0:T(8,128)(2,1)}), bf16[336,168]{1,0:T(8,128)(2,1)}) %reduce-scatter.13.cloned.1.call-update) | async-done | bytes 112912
  347.6 1.0 copy.25
  348.8 9.7 %psum.30 = f32[168]{0:T(256)S(1)} all-reduce(f32[168]{0:T(256)S(1)} %fusion.17), channel_id=1, replica_groups=mesh['row'=4,'col'=8] {'row'}, use_global_device_ids=true, to_apply=%region_7.8 | all-reduce | flops 168 | bytes 1344 | tf_op jit(solution)/shard_map/psum | solution.py:110
  359.4 12.0 %reduce-scatter.15.cloned.1.call-done = bf16[336,168]{1,0:T(8,128)(2,1)} async-done(((bf16[1344,168]{1,0:T(8,128)(2,1)}), bf16[336,168]{1,0:T(8,128)(2,1)}) %reduce-scatter.15.cloned.1.call-update) | async-done | bytes 112912
  371.4 1.0 copy.27
  372.5 11.8 %psum.31 = f32[336]{0:T(512)S(1)} all-reduce(f32[336]{0:T(512)S(1)} %fusion.20), channel_id=1, replica_groups=mesh['row'=4,'col'=8] {'col'}, use_global_device_ids=true, to_apply=%region_11.12 | all-reduce | flops 336 | bytes 2688 | tf_op jit(solution)/shard_map/psum | solution.py:111
  (60 shorter events, 7.3 us)
Async XLA Ops:
  7.2 130.1 %all-gather.3.cloned.1.call-start = ((), (), s32[]{:S(2)}) async-start(), calls=%async_computation.6 | async-start | bytes 4730880 | tf_op jit(solution)/shard_map/all_gather | solution.py:75
  33.8 1.9 copy-start.1
  35.6 174.2 %all-gather.5.cloned.1.call-start = ((), (), s32[]{:S(2)}) async-start(), calls=%async_computation.7 | async-start | bytes 4730880 | tf_op jit(solution)/shard_map/all_gather | solution.py:76
  60.3 1.8 copy-start.2
  62.3 4.4 %copy-start.3 = (f32[336,1024]{1,0:T(8,128)S(1)}, f32[336,1024]{1,0:T(8,128)}, u32[]{:S(2)}) copy-start(f32[336,1024]{1,0:T(8,128)} %param.7) | copy-start | bytes 4128772
  63.2 42.7 %all-to-all-start = ((bf16[336,4,256]{2,0,1:T(8,128)(2,1)}), bf16[336,4,256]{2,0,1:T(8,128)(2,1)S(1)}, u32[]{:S(2)}, u32[]{:S(2)}) async-start(bf16[336,4,256]{2,0,1:T(8,128)(2,1)} %bitcast.108), calls=%async_computation | async-start | bytes 1376256 | tf_op jit(solution)/shard_map/all_to_all | solution.py:52
  66.8 43.3 %copy-start.6 = (s32[32]{0:T(128)S(1)}, s32[32]{0:T(128)}, u32[]{:S(2)}) copy-start(s32[32]{0:T(128)} %param.8) | copy-start | bytes 388
  105.9 30.1 %all-to-all-start.1 = ((bf16[336,4,256]{2,0,1:T(8,128)(2,1)}), bf16[336,4,256]{2,0,1:T(8,128)(2,1)S(1)}, u32[]{:S(2)}, u32[]{:S(2)}) async-start(bf16[336,4,256]{2,0,1:T(8,128)(2,1)} %bitcast.107), calls=%async_computation.1 | async-start | bytes 1376256 | tf_op jit(solution)/shard_map/all_to_all | solution.py:55
  109.4 161.3 %reduce-scatter.17.cloned.1.call-start = ((), (), s32[]{:S(2)}) async-start(), calls=%async_computation.10 | async-start | bytes 4257792
  137.3 5.1 %copy-start.7 = (f32[1,32,1344]{2,1,0:T(8,128)S(1)}, f32[1,32,1344]{2,1,0:T(8,128)}, u32[]{:S(2)}) copy-start(f32[1,32,1344]{2,1,0:T(8,128)} %param.9) | copy-start | bytes 516100
  141.3 1.1 copy-start.8
  142.4 67.4 %copy-start.4 = (bf16[1344,256]{1,0:T(8,128)(2,1)S(1)}, bf16[1344,256]{1,0:T(8,128)(2,1)}, u32[]{:S(2)}) copy-start(bf16[1344,256]{1,0:T(8,128)(2,1)} %get-tuple-element.7) | copy-start | bytes 2064388
  223.5 1.1 copy-start.5
  223.5 99.2 %reduce-scatter.19.cloned.1.call-start = ((), (), s32[]{:S(2)}) async-start(), calls=%async_computation.11 | async-start | bytes 4257792
  227.8 119.8 %reduce-scatter.13.cloned.1.call-start = ((), (), s32[]{:S(2)}) async-start(), calls=%async_computation.8 | async-start | bytes 860160
  272.9 75.8 %copy-start = (f32[1,336,168]{1,2,0:T(8,128)S(1)}, f32[1,336,168]{1,2,0:T(8,128)}, u32[]{:S(2)}) copy-start(f32[1,336,168]{1,2,0:T(8,128)} %param.10) | copy-start | bytes 677380
  272.9 98.5 %reduce-scatter.15.cloned.1.call-start = ((), (), s32[]{:S(2)}) async-start(), calls=%async_computation.9 | async-start | bytes 860160
Sparse Core Ops, SparseCore 0:
  35.7 99.2 all-gather.2
  136.6 73.1 all-gather.4
  223.6 47.0 reduce-scatter.16
  274.1 48.5 reduce-scatter.18
  324.8 22.7 reduce-scatter.12
  349.8 21.5 reduce-scatter.14
where the time goes:
time: 393 us; the launch traced here: 392 us
  waiting for transfers between devices  235 us (60%)
  blocking collectives  70.5 us (18%)
  other arithmetic  25.9 us (7%)
  matrix products  23 us (6%)
  local copies, waits for them, and re-layouts  15.4 us (4%)
  between operations  14.3 us (4%)
  starting transfers between devices  7.4 us (2%)
    unnamed x10, waiting for transfers between devices  127 us
    all_gather x1, waiting for transfers between devices, local(): lax.all_gather(part_second, 'row', axis=1, tiled=True)  65.3 us
    all_to_all x1, waiting for transfers between devices, local(): lax.all_to_all(clean.astype(jnp.bfloat16), 'row', split_axis=1, concat_ax...  38.2 us
    div x1, other arithmetic, local(): 2.0 * levels / spread_root  15.7 us
    psum x1, blocking collectives, local(): lax.psum(jnp.sum(weight_first * weight_first, axis=0), 'row') + 1.0  13.5 us
    psum x1, blocking collectives, local(): lax.psum(jnp.sum(weight_second * weight_second, axis=0), 'col') + 1.0  13.3 us
    psum x1, blocking collectives, local(): dot_second = lax.psum(jnp.sum(weight_second * gsecond, axis=0), 'col')  11.8 us
    all_gather x1, blocking collectives, local(): lax.all_gather(normed_second, 'col', axis=0, tiled=True)  11.3 us
  transfers between devices with their start and end apart: 8, of which 7 were waited for; matrix products, arithmetic and copies ran while one was open for 11% of the time, Pallas kernels for 0%

commit v1 on v0

--- a/solution.py
+++ b/solution.py
@@ -3,6 +3,8 @@
 import jax
 import jax.numpy as jnp
 from jax import lax
+from jax.experimental import pallas as pl
+from jax.experimental.pallas import tpu as pltpu
 from jax.sharding import PartitionSpec as P
 
 PIX = 256
@@ -116,6 +118,370 @@
     return (grad_first[None], grad_second[None])
 
 
+CORES = 2
+SIDE = 2
+MESH = pl.DeviceIdType.MESH
+(S_UP, S_DN, S_X, S_Y, S_D0, S_D1, S_S, S_T, S_F, R_Z, R_X, R_Y, R_D0, R_D1, R_S, R_T, R_F,
+ S_A0, S_A1, R_A0, R_A1, S_BX, S_CX, S_BY, S_CY, R_BX, R_CX, R_BY, R_CY, S_P, R_P, MISC) = range(32)
+
+
+def round_up(size, unit):
+    return -(-size // unit) * unit
+
+
+def step_kernel(
+    hb, ib, samples, wown, sto, gsel, w1f, w2f, out1, out2,
+    w, st, tg, pre, hid, brp, brk, brr, dbr, db2, dpre, s2, d2, g,
+    ra, sa, rx, ry, pz, rz, colf, sems,
+):
+    rows = st.shape[1] // wown.shape[2]
+    hp, ip = wown.shape[1], wown.shape[2]
+    chips = w.shape[1] // hp
+    sub = st.shape[2]
+    z = lax.axis_index("row")
+    col = lax.axis_index("col")
+    core = lax.rem(col, CORES)
+    xy = col // CORES
+    x, y = lax.rem(xy, SIDE), xy // SIDE
+    xn = y * SIDE + (1 - x)
+    yn = (1 - y) * SIDE + x
+    dn = (1 - y) * SIDE + (1 - x)
+    dev_x = (z, xn * CORES + core)
+    dev_y = (z, yn * CORES + core)
+    dev_p = (z, xy * CORES + 1 - core)
+    up, down = (z + 1, col), (z - 1, col)
+    ring = [lax.rem(z + k, rows) for k in range(rows)]
+
+    barrier = pltpu.get_barrier_semaphore()
+    peers = [dev_x, dev_y, dev_p] + [(ring[k], col) for k in range(1, rows)]
+    for peer in peers:
+        pl.semaphore_signal(barrier, inc=1, device_id=peer, device_id_type=MESH)
+
+    pending = []
+
+    def remote(src, dst, send, recv, dev):
+        return pltpu.make_async_remote_copy(
+            src_ref=src, dst_ref=dst, send_sem=sems.at[send[0], send[1]],
+            recv_sem=sems.at[recv[0], recv[1]], device_id=dev, device_id_type=MESH,
+        )
+
+    def when(cond, fn):
+        if cond is None:
+            fn()
+        else:
+            pl.when(cond)(fn)
+
+    def send(cond, *spec):
+        when(cond, lambda: remote(*spec).start())
+        pending.append((cond, spec))
+
+    def arrive(cond, dst, recv):
+        when(cond, lambda: remote(dst, dst, recv, recv, dev_p).wait_recv())
+
+    def both(a, b):
+        return b if a is None else (a if b is None else jnp.logical_and(a, b))
+
+    def blk(zb, xyb, half=None):
+        at = (pl.ds(pl.multiple_of(xyb * hp, 16), hp), pl.ds(pl.multiple_of(zb * ip, 128), ip))
+        return w.at[(slice(None),) + at] if half is None else w.at[(half,) + at]
+
+    def chan(zb):
+        return pl.ds(pl.multiple_of(zb * ip, 128), ib)
+
+    def pix(zb):
+        return pl.ds(pl.multiple_of(zb * sub, 128), sub)
+
+    local_w = pltpu.make_async_copy(wown, blk(z, xy), sems.at[MISC, 0])
+    local_w.start()
+    local_s = pltpu.make_async_copy(sto.at[0, :, pix(z)], st.at[core, chan(z)], sems.at[MISC, 1])
+    local_s.start()
+    local_t = pltpu.make_async_copy(sto.at[1, :, pix(z)], tg.at[chan(z)], sems.at[MISC, 2])
+    local_t.start()
+    for zb in range(rows):
+        pad = slice(zb * ip + ib, (zb + 1) * ip)
+        zero = jnp.zeros((ip - ib, sub), jnp.bfloat16)
+        st[0, pad, :] = zero
+        st[1, pad, :] = zero
+        tg[pad, :] = zero
+    pl.semaphore_wait(barrier, len(peers))
+
+    def spread(cond, zb, src, go_up, go_down):
+        if go_up:
+            send(both(cond, z + 1 < rows), src, blk(zb, xy), (S_UP, zb), (R_Z, zb), up)
+        if go_down:
+            send(both(cond, z > 0), src, blk(zb, xy), (S_DN, zb), (R_Z, zb), down)
+        send(cond, src, blk(zb, xy), (S_X, zb), (R_X, zb), dev_x)
+        send(cond, src, blk(zb, xy), (S_Y, zb), (R_Y, zb), dev_y)
+
+    def state_out(k):
+        zt = ring[k]
+        send(None, sto.at[0, :, pix(zt)], st.at[core, chan(z)], (S_S, k), (R_S, z), (zt, col))
+
+    def diagonal(cond, zb):
+        arrive(cond, blk(zb, xn), (R_X, zb))
+        send(cond, blk(zb, xn, 0), blk(zb, xn, 0), (S_D0, zb), (R_D0, zb), dev_y)
+        arrive(cond, blk(zb, yn), (R_Y, zb))
+        send(cond, blk(zb, yn, 1), blk(zb, yn, 1), (S_D1, zb), (R_D1, zb), dev_x)
+
+    spread(None, z, wown, True, True)
+    send(None, sto.at[0, :, pix(z)], st.at[core, chan(z)], (S_F, z), (R_F, z), dev_p)
+    for d in range(1, rows + 1):
+        if d < rows:
+            state_out(d)
+            low, high = z - d, z + d
+            arrive(low >= 0, blk(low, xy), (R_Z, low))
+            spread(low >= 0, low, blk(low, xy), True, False)
+            arrive(high < rows, blk(high, xy), (R_Z, high))
+            spread(high < rows, high, blk(high, xy), False, True)
+        if d == 1:
+            diagonal(None, z)
+        else:
+            diagonal(z - (d - 1) >= 0, z - (d - 1))
+            diagonal(z + (d - 1) < rows, z + (d - 1))
+        if d == rows - 1:
+            for k in range(1, rows):
+                zt = ring[k]
+                send(None, sto.at[1, :, pix(zt)], tg.at[chan(z)], (S_T, k), (R_T, z), (zt, col))
+    for k in range(1, rows):
+        zb = ring[rows - k]
+        arrive(None, st.at[core, chan(zb)], (R_S, zb))
+        send(None, st.at[core, chan(zb)], st.at[core, chan(zb)], (S_F, zb), (R_F, zb), dev_p)
+    for zb in range(rows):
+        arrive(None, blk(zb, dn, 0), (R_D0, zb))
+        arrive(None, blk(zb, dn, 1), (R_D1, zb))
+    local_w.wait()
+    local_s.wait()
+    local_t.wait()
+
+    half_rows = w.shape[1] // 2
+    for part in range(2):
+        at = slice(part * half_rows, (part + 1) * half_rows)
+        block = w[0, at, :].astype(jnp.float32)
+        colf[at, :] = jnp.broadcast_to(
+            jnp.sqrt(1.0 + jnp.sum(block * block, axis=1, keepdims=True)), (half_rows, colf.shape[1])
+        )
+    total = jnp.zeros((1, w.shape[2]), jnp.float32)
+    for part in range(2):
+        block = w[1, part * half_rows : (part + 1) * half_rows, :].astype(jnp.float32)
+        total = total + jnp.sum(block * block, axis=0, keepdims=True)
+    s2[0] = jnp.broadcast_to(total, s2.shape[1:])
+    send(None, s2.at[0], s2.at[1], (MISC, 3), (MISC, 4), dev_p)
+    for zb in range(rows):
+        arrive(None, st.at[1 - core, chan(zb)], (R_F, zb))
+
+    def forward(j):
+        @pl.loop(0, 2)
+        def _(part):
+            at = pl.ds(pl.multiple_of(part * half_rows, 16), half_rows)
+            value = jnp.dot(w[0, at, :], st[j], preferred_element_type=jnp.float32)
+            value = value / colf[at, :1]
+            pre[j, at, :] = value
+            hid[j, at, :] = (value * jax.nn.sigmoid(value) * SILU_GAIN * gsel[j, at, :]).astype(jnp.bfloat16)
+
+    def branch_part(j, dst):
+        @pl.loop(0, rows)
+        def _(zb):
+            at = pl.ds(pl.multiple_of(zb * ip, 128), ip)
+            dst[at, :] = lax.dot_general(
+                w[1, :, at], hid[j], CONTRACT_LEAD, preferred_element_type=jnp.float32
+            )
+
+    forward(1 - core)
+    branch_part(1 - core, brp)
+    send(None, brp, brr, (MISC, 5), (MISC, 6), dev_p)
+    forward(core)
+    branch_part(core, brk)
+    for k in range(1, rows):
+        arrive(None, tg.at[chan(ring[k])], (R_T, ring[k]))
+    arrive(None, s2.at[1], (MISC, 4))
+    col2_row = jnp.sqrt(1.0 + s2[0] + s2[1])
+    col2 = col2_row.T[:, :1]
+    arrive(None, brr, (MISC, 6))
+    for zb in range(rows):
+        at = slice(zb * ip, (zb + 1) * ip)
+        norm = col2[at, :]
+        branch = (brk[at, :] + brr[at, :]) / norm
+        fresh = (KEEP_COEF * st[core, at, :].astype(jnp.float32) + ADD_COEF * branch).astype(jnp.bfloat16)
+        slope = (fresh.astype(jnp.float32) - tg[at, :].astype(jnp.float32)) / samples
+        rounded = (ADD_COEF * slope).astype(jnp.bfloat16)
+        dbr[core, at, :] = rounded
+        product = jnp.sum(branch * rounded.astype(jnp.float32), axis=1, keepdims=True) * norm
+        d2[0, :, at] = jnp.broadcast_to(product, (ip, 128)).T[: d2.shape[1], :]
+    send(None, dbr.at[core], dbr.at[core], (MISC, 7), (MISC, 8), dev_p)
+    send(None, d2.at[0], d2.at[1], (MISC, 9), (MISC, 10), dev_p)
+
+    def scale_back(j):
+        for zb in range(rows):
+            at = slice(zb * ip, (zb + 1) * ip)
+            db2[j, at, :] = (dbr[j, at, :].astype(jnp.float32) / col2[at, :]).astype(jnp.bfloat16)
+
+    def backward(j):
+        @pl.loop(0, 2)
+        def _(part):
+            at = pl.ds(pl.multiple_of(part * half_rows, 16), half_rows)
+            grad = jnp.dot(w[1, at, :], db2[j], preferred_element_type=jnp.float32)
+            dpre[j, at, :] = (grad * gsel[j, at, :] * silu_slope(pre[j, at, :]) * SILU_GAIN).astype(jnp.bfloat16)
+
+    scale_back(core)
+    backward(core)
+    arrive(None, dbr.at[1 - core], (MISC, 8))
+    arrive(None, d2.at[1], (MISC, 10))
+    scale_back(1 - core)
+    backward(1 - core)
+    dot1 = colf[:, :1] * sum(
+        jnp.sum(dpre[j].astype(jnp.float32) * pre[j], axis=1, keepdims=True) for j in range(CORES)
+    )
+    lane = lax.broadcasted_iota(jnp.int32, (1, ip), 1)
+    line = lax.broadcasted_iota(jnp.int32, (hp, 1), 0)
+
+    def gradients(zb):
+        at = pl.ds(pl.multiple_of(zb * ip, 128), ip)
+        first = sum(
+            lax.dot_general(dpre[j], st[j, at, :], CONTRACT_TAIL, preferred_element_type=jnp.float32)
+            for j in range(CORES)
+        )
+        g[0, :, at] = jnp.where(lane >= ib, dot1, first).astype(jnp.bfloat16)
+        second = sum(
+            lax.dot_general(hid[j], dbr[j, at, :], CONTRACT_TAIL, preferred_element_type=jnp.float32)
+            for j in range(CORES)
+        )
+        dot2 = d2[0, :1, at] + d2[1, :1, at]
+        for b in range(chips):
+            part = second[b * hp : (b + 1) * hp, :]
+            g[1, b * hp : (b + 1) * hp, at] = jnp.where(line >= hb, dot2, part).astype(jnp.bfloat16)
+
+    def gblk(half, xyb, zb):
+        return (half, pl.ds(pl.multiple_of(xyb * hp, 16), hp), pl.ds(pl.multiple_of(zb * ip, 128), ip))
+
+    order = ring[1:] + ring[:1]
+
+    def stage_a(k):
+        zb = order[k]
+        send(None, g.at[gblk(0, dn, zb)], ra.at[0, k], (S_A0, k), (R_A0, k), dev_y)
+        send(None, g.at[gblk(1, dn, zb)], ra.at[1, k], (S_A1, k), (R_A1, k), dev_x)
+        send(None, g.at[gblk(1, xn, zb)], rx.at[1, k], (S_CX, k), (R_CX, k), dev_x)
+        send(None, g.at[gblk(0, yn, zb)], ry.at[0, k], (S_CY, k), (R_CY, k), dev_y)
+
+    def wide(value):
+        return value.astype(jnp.float32)
+
+    def stage_b(k):
+        zb = order[k]
+        arrive(None, ra.at[0, k], (R_A0, k))
+        sa[0, k] = (wide(g[gblk(0, xn, zb)]) + wide(ra[0, k])).astype(jnp.bfloat16)
+        send(None, sa.at[0, k], rx.at[0, k], (S_BX, k), (R_BX, k), dev_x)
+        arrive(None, ra.at[1, k], (R_A1, k))
+        sa[1, k] = (wide(g[gblk(1, yn, zb)]) + wide(ra[1, k])).astype(jnp.bfloat16)
+        send(None, sa.at[1, k], ry.at[1, k], (S_BY, k), (R_BY, k), dev_y)
+
+    def stage_c(k):
+        zb = order[k]
+        arrive(None, rx.at[1, k], (R_CX, k))
+        arrive(None, ry.at[0, k], (R_CY, k))
+        arrive(None, rx.at[0, k], (R_BX, k))
+        arrive(None, ry.at[1, k], (R_BY, k))
+        sums = [wide(g[gblk(half, xy, zb)]) + wide(rx[half, k]) + wide(ry[half, k]) for half in range(2)]
+        if k == rows - 1:
+            return sums
+        pz[k, 0] = sums[0].astype(jnp.bfloat16)
+        pz[k, 1] = sums[1].astype(jnp.bfloat16)
+        send(None, pz.at[k], rz.at[k], (S_P, k), (R_P, k), (zb, col))
+        return None
+
+    for k in range(rows):
+        gradients(order[k])
+        stage_a(k)
+        if k >= 1:
+            stage_b(k - 1)
+    sums = None
+    for k in range(rows):
+        if k == rows - 2:
+            stage_b(rows - 1)
+        sums = stage_c(k)
+    for k in range(rows - 1):
+        arrive(None, rz.at[k], (R_P, k))
+    first, second = (
+        sums[half] + sum(wide(rz[k, half]) for k in range(rows - 1)) for half in range(2)
+    )
+    norm1 = colf[pl.ds(pl.multiple_of(xy * hp, 16), hp), :1][:hb]
+    dot_first = first[:hb, ib : ib + 1]
+    out1[...] = first[:hb, :ib] / norm1 - w1f[...] * (dot_first / (norm1 * norm1 * norm1))
+    mine = pl.ds(pl.multiple_of(z * ip, 128), ip)
+    norm2 = jnp.sqrt(1.0 + s2[0, :1, mine] + s2[1, :1, mine])[:, :ib]
+    dot_second = second[hb : hb + 1, :ib]
+    out2[...] = second[:hb, :ib] / norm2 - w2f[...] * (dot_second / (norm2 * norm2 * norm2))
+    for cond, spec in pending:
+        when(cond, lambda spec=spec: remote(*spec).wait_send())
+
+
+def local_step(clean, noise, bucket, mod_table, w_first, w_second):
+    rows = lax.axis_size("row")
+    cols = lax.axis_size("col")
+    z, col = lax.axis_index("row"), lax.axis_index("col")
+    samples = bucket.shape[0]
+    own_rows = clean.shape[1]
+    ib, hb = clean.shape[0], w_first.shape[2]
+    sub = own_rows // rows
+    if sub != PIX:
+        return local(clean, noise, bucket, mod_table, w_first, w_second)
+    chips = cols // CORES
+    hp, ip = round_up(hb + 1, 16), round_up(ib + 1, 128)
+    bf16 = jnp.bfloat16
+    w1f, w2f = w_first[0].T, w_second[0]
+    wown = jnp.stack([w1f, w2f]).astype(bf16)
+    wown = jnp.pad(wown, ((0, 0), (0, hp - hb), (0, ip - ib)))
+    sample = lax.dynamic_slice_in_dim(bucket, col * rows, rows)
+    levels = jnp.repeat(noise_levels(sample), PIX)[None, :]
+    root = jnp.sqrt(levels * levels + 0.25)
+    sto = jnp.stack([
+        ((clean + levels * noise) / root).astype(bf16),
+        (clean * (2.0 * levels / root) - noise * (0.5 / root)).astype(bf16),
+    ])
+    chip = col // CORES
+    picked = jnp.stack([lax.dynamic_index_in_dim(bucket, (chip * CORES + j) * rows + z, keepdims=False) for j in range(CORES)])
+    table = mod_table[0].reshape(mod_table.shape[1], chips, CORES, hb)
+    mine = lax.dynamic_index_in_dim(table, lax.rem(col, CORES), axis=2, keepdims=False)
+    gsel = 1.0 + jnp.take(mine, picked, axis=0)
+    gsel = jnp.pad(gsel, ((0, 0), (0, 0), (0, hp - hb))).reshape(CORES, chips * hp, 1)
+    hh, ii = chips * hp, rows * ip
+    f32 = jnp.float32
+    vmem = pl.BlockSpec(memory_space=pltpu.VMEM)
+    out1, out2 = pl.pallas_call(
+        lambda *refs: step_kernel(hb, ib, samples, *refs),
+        out_shape=(jax.ShapeDtypeStruct((hb, ib), f32), jax.ShapeDtypeStruct((hb, ib), f32)),
+        in_specs=[vmem] * 5,
+        out_specs=(vmem, vmem),
+        scratch_shapes=[
+            pltpu.VMEM((2, hh, ii), bf16),
+            pltpu.VMEM((2, ii, sub), bf16),
+            pltpu.VMEM((ii, sub), bf16),
+            pltpu.VMEM((2, hh, sub), f32),
+            pltpu.VMEM((2, hh, sub), bf16),
+            pltpu.VMEM((ii, sub), f32),
+            pltpu.VMEM((ii, sub), f32),
+            pltpu.VMEM((ii, sub), f32),
+            pltpu.VMEM((2, ii, sub), bf16),
+            pltpu.VMEM((2, ii, sub), bf16),
+            pltpu.VMEM((2, hh, sub), bf16),
+            pltpu.VMEM((2, 8, ii), f32),
+            pltpu.VMEM((2, 8, ii), f32),
+            pltpu.VMEM((2, hh, ii), bf16),
+            pltpu.VMEM((2, rows, hp, ip), bf16),
+            pltpu.VMEM((2, rows, hp, ip), bf16),
+            pltpu.VMEM((2, rows, hp, ip), bf16),
+            pltpu.VMEM((2, rows, hp, ip), bf16),
+            pltpu.VMEM((rows, 2, hp, ip), bf16),
+            pltpu.VMEM((rows, 2, hp, ip), bf16),
+            pltpu.VMEM((hh, 128), f32),
+            pltpu.SemaphoreType.DMA((32, max(rows, 11))),
+        ],
+        compiler_params=pltpu.CompilerParams(
+            collective_id=0, has_side_effects=True, vmem_limit_bytes=60 * 1024 * 1024
+        ),
+    )(wown, sto, gsel, w1f, w2f)
+    return (out1.T[None], out2[None])
+
+
 def solution(mesh):
     placed = (
         P("row", "col"),
@@ -126,7 +492,7 @@
         P(None, "col", "row"),
     )
     return jax.shard_map(
-        local,
+        local_step if mesh.shape["col"] == CORES * SIDE * SIDE else local,
         mesh=mesh,
         in_specs=placed,
         out_specs=(P(None, "row", "col"), P(None, "col", "row")),

time: 393 us -> 128 us (0.33)
  the two profiles are of different devices: /device:TPU:0 before, /device:TPU:11 now
where the time goes in v1:
time: 128 us
  Pallas kernels  113 us (88%)
  other arithmetic  7.77 us (6%)
  local copies, waits for them, and re-layouts  6.38 us (5%)
    pallas_call x1, Pallas kernels, local_step(): pl.pallas_call(lambda *refs: step_kernel(hb, ib, samples, *refs), out_sha...  113 us
    unnamed x13, local copies, waits for them, and re-layouts  3.46 us
    another operation x2, other arithmetic, local_step(): jnp.stack([((clean + levels * noise) / root).astype(bf16), (clean * (2.0...  3.41 us

profile of v1, /device:TPU:11, one launch (start us, length us, event | category | flops | bytes accessed | tf_op | source)
XLA Modules:
  0.0 128.1 jit_solution(14588953375046994842)
XLA Ops:
  0.6 0.7 add_exponential_fusion
  1.4 0.1 broadcast_bitcast_fusion
  1.5 2.2 %fusion.1 = (bf16[1,336,1024]{2,1,0:T(8,128)(2,1)S(1)}, bf16[1,336,1024]{2,1,0:T(8,128)(2,1)S(1)}) fusion(f32[1024]{0:T(1024)S(1)} %get-tuple-element.8, f32[336,1024]{1,0:T(8,128)} %param.6, f32[336,1024]{1,0:T(8,128)} %param.7, f32[1024]{0:T(1024)S(1)} %bitcast.31, f32[1024]{0:T(1024)S(1)} %get-tuple-element.9, f32[1024]{0:T(1024)S(1)} %get-tuple-element.10), kind=kLoop, calls=%fused_computation.5 | loop fusion | flops 2752512 | bytes 4145152 | tf_op jit(solution)/shard_map/stack | solution.py:436
  3.7 0.0 copy-start.3
  3.7 0.0 copy-start.2
  3.7 1.2 pad_maximum_fusion.refs_1_
  4.9 0.0 copy-start
  4.9 0.0 copy-start.1
  4.9 0.0 copy-done.3
  4.9 0.6 fusion.10
  5.5 1.4 %fusion.9 = s32[2]{0:T(128)S(1)} fusion(s32[1,1]{0,1:T(1,128)} %bitcast.6, s32[1,1]{0,1:T(1,128)} %bitcast.5), kind=kLoop, calls=%fused_computation.26 | loop fusion | flops 8 | bytes 16 | tf_op jit(solution)/shard_map/jit(_take)/jit(_where)/select_n | solution.py:444
  6.9 0.0 copy-done.2
  6.9 0.5 reshape_squeeze.3
  7.4 0.1 constant_dynamic-slice_fusion
  7.5 0.6 gather_fusion
  8.1 1.4 %compare_and_fusion = pred[2]{0:T(512)(128)(4,1)S(1)} fusion(s32[1]{0:T(128)} %get-tuple-element.12, s32[1]{0:T(128)} %get-tuple-element.11), kind=kLoop, calls=%fused_computation.25 | loop fusion | flops 14 | bytes 10 | tf_op jit(solution)/shard_map/jit(_take)/and | solution.py:444
  9.5 0.1 select_add_fusion
  9.6 1.2 reshape.139.refs_2_
  10.7 0.0 copy-done
  10.8 0.0 copy-done.1
  10.8 0.7 fusion.7.refs_0_
  11.5 113.2 %shard_map.77 = (f32[168,336]{1,0:T(8,128)}, f32[168,336]{1,0:T(8,128)}) custom-call(bf16[2,176,384]{2,1,0:T(8,128)(2,1)} %fusion.7.refs_0_, bf16[2,336,1024]{2,1,0:T(8,128)(2,1)} %pad_maximum_fusion.refs_1_, f32[2,704,1]{2,1,0:T(8,128)} %reshape.139.refs_2_, f32[168,336]{1,0:T(8,128)} %bitcast.26, f32[168,336]{1,0:T(8,128)} %bitcast.25), custom_call_target="tpu_custom_call" | custom-call | tf_op jit(solution)/shard_map/pallas_call | solution.py:449
  124.7 1.7 %copy.15 = f32[1,336,168]{1,2,0:T(8,128)} copy(f32[1,336,168]{1,2,0:T(8,128)} %bitcast.28) | data formatting | bytes 451584
  126.4 1.7 %copy.16 = f32[1,168,336]{2,1,0:T(8,128)} copy(f32[1,168,336]{2,1,0:T(8,128)} %bitcast.27) | data formatting | bytes 451584
  (7 shorter events, 0.1 us)
Async XLA Ops:
  3.7 1.3 copy-start.3
  3.7 3.2 %copy-start.2 = (f32[1,32,1344]{2,1,0:T(8,128)S(1)}, f32[1,32,1344]{2,1,0:T(8,128)}, u32[]{:S(2)}) copy-start(f32[1,32,1344]{2,1,0:T(8,128)} %param.9) | copy-start | bytes 516100
  4.9 5.8 %copy-start = (f32[1,168,336]{2,1,0:T(8,128)S(1)}, f32[1,168,336]{2,1,0:T(8,128)}, u32[]{:S(2)}) copy-start(f32[1,168,336]{2,1,0:T(8,128)} %param.11) | copy-start | bytes 677380
  4.9 5.8 %copy-start.1 = (f32[1,336,168]{1,2,0:T(8,128)S(1)}, f32[1,336,168]{1,2,0:T(8,128)}, u32[]{:S(2)}) copy-start(f32[1,336,168]{1,2,0:T(8,128)} %param.10) | copy-start | bytes 677380

commit v2 on v1

--- a/solution.py
+++ b/solution.py
@@ -132,7 +132,7 @@
 def step_kernel(
     hb, ib, samples, wown, sto, gsel, w1f, w2f, out1, out2,
     w, st, tg, pre, hid, brp, brk, brr, dbr, db2, dpre, s2, d2, g,
-    ra, sa, rx, ry, pz, rz, colf, sems,
+    ra, sa, rx, ry, pz, rz, colf, gcol, sems,
 ):
     rows = st.shape[1] // wown.shape[2]
     hp, ip = wown.shape[1], wown.shape[2]
@@ -225,23 +225,24 @@
 
     spread(None, z, wown, True, True)
     send(None, sto.at[0, :, pix(z)], st.at[core, chan(z)], (S_F, z), (R_F, z), dev_p)
+    for k in range(1, rows):
+        state_out(k)
     for d in range(1, rows + 1):
         if d < rows:
-            state_out(d)
             low, high = z - d, z + d
             arrive(low >= 0, blk(low, xy), (R_Z, low))
             spread(low >= 0, low, blk(low, xy), True, False)
             arrive(high < rows, blk(high, xy), (R_Z, high))
             spread(high < rows, high, blk(high, xy), False, True)
         if d == 1:
+            for k in range(1, rows):
+                zt = ring[k]
+                send(None, sto.at[1, :, pix(zt)], tg.at[chan(z)], (S_T, k), (R_T, z), (zt, col))
+        if d == 1:
             diagonal(None, z)
         else:
             diagonal(z - (d - 1) >= 0, z - (d - 1))
             diagonal(z + (d - 1) < rows, z + (d - 1))
-        if d == rows - 1:
-            for k in range(1, rows):
-                zt = ring[k]
-                send(None, sto.at[1, :, pix(zt)], tg.at[chan(z)], (S_T, k), (R_T, z), (zt, col))
     for k in range(1, rows):
         zb = ring[rows - k]
         arrive(None, st.at[core, chan(zb)], (R_S, zb))
@@ -254,6 +255,8 @@
     local_t.wait()
 
     half_rows = w.shape[1] // 2
+    for j in range(CORES):
+        gcol[j] = gsel[j].T
     for part in range(2):
         at = slice(part * half_rows, (part + 1) * half_rows)
         block = w[0, at, :].astype(jnp.float32)
@@ -276,7 +279,7 @@
             value = jnp.dot(w[0, at, :], st[j], preferred_element_type=jnp.float32)
             value = value / colf[at, :1]
             pre[j, at, :] = value
-            hid[j, at, :] = (value * jax.nn.sigmoid(value) * SILU_GAIN * gsel[j, at, :]).astype(jnp.bfloat16)
+            hid[j, at, :] = (value * jax.nn.sigmoid(value) * SILU_GAIN * gcol[j, at, :1]).astype(jnp.bfloat16)
 
     def branch_part(j, dst):
         @pl.loop(0, rows)
@@ -320,27 +323,24 @@
         def _(part):
             at = pl.ds(pl.multiple_of(part * half_rows, 16), half_rows)
             grad = jnp.dot(w[1, at, :], db2[j], preferred_element_type=jnp.float32)
-            dpre[j, at, :] = (grad * gsel[j, at, :] * silu_slope(pre[j, at, :]) * SILU_GAIN).astype(jnp.bfloat16)
+            dpre[j, at, :] = (grad * gcol[j, at, :1] * silu_slope(pre[j, at, :]) * SILU_GAIN).astype(jnp.bfloat16)
 
     scale_back(core)
     backward(core)
     arrive(None, dbr.at[1 - core], (MISC, 8))
     arrive(None, d2.at[1], (MISC, 10))
-    scale_back(1 - core)
-    backward(1 - core)
-    dot1 = colf[:, :1] * sum(
-        jnp.sum(dpre[j].astype(jnp.float32) * pre[j], axis=1, keepdims=True) for j in range(CORES)
-    )
     lane = lax.broadcasted_iota(jnp.int32, (1, ip), 1)
     line = lax.broadcasted_iota(jnp.int32, (hp, 1), 0)
-
-    def gradients(zb):
-        at = pl.ds(pl.multiple_of(zb * ip, 128), ip)
-        first = sum(
-            lax.dot_general(dpre[j], st[j, at, :], CONTRACT_TAIL, preferred_element_type=jnp.float32)
-            for j in range(CORES)
-        )
-        g[0, :, at] = jnp.where(lane >= ib, dot1, first).astype(jnp.bfloat16)
+    order = ring[1:] + ring[:1]
+
+    def gblk(half, xyb, zb):
+        return (half, pl.ds(pl.multiple_of(xyb * hp, 16), hp), pl.ds(pl.multiple_of(zb * ip, 128), ip))
+
+    def wide(value):
+        return value.astype(jnp.float32)
+
+    for k in range(rows):
+        at = pl.ds(pl.multiple_of(order[k] * ip, 128), ip)
         second = sum(
             lax.dot_general(hid[j], dbr[j, at, :], CONTRACT_TAIL, preferred_element_type=jnp.float32)
             for j in range(CORES)
@@ -349,30 +349,34 @@
         for b in range(chips):
             part = second[b * hp : (b + 1) * hp, :]
             g[1, b * hp : (b + 1) * hp, at] = jnp.where(line >= hb, dot2, part).astype(jnp.bfloat16)
-
-    def gblk(half, xyb, zb):
-        return (half, pl.ds(pl.multiple_of(xyb * hp, 16), hp), pl.ds(pl.multiple_of(zb * ip, 128), ip))
-
-    order = ring[1:] + ring[:1]
+        send(None, g.at[gblk(1, dn, order[k])], ra.at[1, k], (S_A1, k), (R_A1, k), dev_x)
+    for k in range(rows):
+        send(None, g.at[gblk(1, xn, order[k])], rx.at[1, k], (S_CX, k), (R_CX, k), dev_x)
+    scale_back(1 - core)
+    backward(1 - core)
+    dot1 = colf[:, :1] * sum(
+        jnp.sum(dpre[j].astype(jnp.float32) * pre[j], axis=1, keepdims=True) for j in range(CORES)
+    )
 
     def stage_a(k):
         zb = order[k]
+        at = pl.ds(pl.multiple_of(zb * ip, 128), ip)
+        first = sum(
+            lax.dot_general(dpre[j], st[j, at, :], CONTRACT_TAIL, preferred_element_type=jnp.float32)
+            for j in range(CORES)
+        )
+        g[0, :, at] = jnp.where(lane >= ib, dot1, first).astype(jnp.bfloat16)
         send(None, g.at[gblk(0, dn, zb)], ra.at[0, k], (S_A0, k), (R_A0, k), dev_y)
-        send(None, g.at[gblk(1, dn, zb)], ra.at[1, k], (S_A1, k), (R_A1, k), dev_x)
-        send(None, g.at[gblk(1, xn, zb)], rx.at[1, k], (S_CX, k), (R_CX, k), dev_x)
+        arrive(None, ra.at[1, k], (R_A1, k))
+        sa[1, k] = (wide(g[gblk(1, yn, zb)]) + wide(ra[1, k])).astype(jnp.bfloat16)
+        send(None, sa.at[1, k], ry.at[1, k], (S_BY, k), (R_BY, k), dev_y)
         send(None, g.at[gblk(0, yn, zb)], ry.at[0, k], (S_CY, k), (R_CY, k), dev_y)
-
-    def wide(value):
-        return value.astype(jnp.float32)
 
     def stage_b(k):
         zb = order[k]
         arrive(None, ra.at[0, k], (R_A0, k))
         sa[0, k] = (wide(g[gblk(0, xn, zb)]) + wide(ra[0, k])).astype(jnp.bfloat16)
         send(None, sa.at[0, k], rx.at[0, k], (S_BX, k), (R_BX, k), dev_x)
-        arrive(None, ra.at[1, k], (R_A1, k))
-        sa[1, k] = (wide(g[gblk(1, yn, zb)]) + wide(ra[1, k])).astype(jnp.bfloat16)
-        send(None, sa.at[1, k], ry.at[1, k], (S_BY, k), (R_BY, k), dev_y)
 
     def stage_c(k):
         zb = order[k]
@@ -389,7 +393,6 @@
         return None
 
     for k in range(rows):
-        gradients(order[k])
         stage_a(k)
         if k >= 1:
             stage_b(k - 1)
@@ -438,11 +441,15 @@
         (clean * (2.0 * levels / root) - noise * (0.5 / root)).astype(bf16),
     ])
     chip = col // CORES
-    picked = jnp.stack([lax.dynamic_index_in_dim(bucket, (chip * CORES + j) * rows + z, keepdims=False) for j in range(CORES)])
-    table = mod_table[0].reshape(mod_table.shape[1], chips, CORES, hb)
-    mine = lax.dynamic_index_in_dim(table, lax.rem(col, CORES), axis=2, keepdims=False)
-    gsel = 1.0 + jnp.take(mine, picked, axis=0)
-    gsel = jnp.pad(gsel, ((0, 0), (0, 0), (0, hp - hb))).reshape(CORES, chips * hp, 1)
+    table = mod_table.reshape(mod_table.shape[1], chips, CORES, hb)
+    picked = [
+        lax.dynamic_slice(
+            table, (bucket[(chip * CORES + j) * rows + z], 0, lax.rem(col, CORES), 0), (1, chips, 1, hb)
+        )[0, :, 0]
+        for j in range(CORES)
+    ]
+    gsel = jnp.pad(1.0 + jnp.stack(picked), ((0, 0), (0, 0), (0, hp - hb)))
+    gsel = jnp.broadcast_to(gsel.reshape(CORES, 1, chips * hp), (CORES, 8, chips * hp))
     hh, ii = chips * hp, rows * ip
     f32 = jnp.float32
     vmem = pl.BlockSpec(memory_space=pltpu.VMEM)
@@ -473,6 +480,7 @@
             pltpu.VMEM((rows, 2, hp, ip), bf16),
             pltpu.VMEM((rows, 2, hp, ip), bf16),
             pltpu.VMEM((hh, 128), f32),
+            pltpu.VMEM((CORES, hh, 8), f32),
             pltpu.SemaphoreType.DMA((32, max(rows, 11))),
         ],
         compiler_params=pltpu.CompilerParams(

time: 128 us -> 142 us (1.11)
  the two profiles are of different devices: /device:TPU:11 before, /device:TPU:0 now
where the time goes in v2:
time: 142 us; the launch traced here: 141 us
  Pallas kernels  125 us (88%)
  local copies, waits for them, and re-layouts  6.9 us (5%)
  other arithmetic  4.95 us (3%)
  between operations  4.64 us (3%)
    pallas_call x1, Pallas kernels, local_step(): pl.pallas_call(lambda *refs: step_kernel(hb, ib, samples, *refs), out_sha...  125 us
    unnamed x9, local copies, waits for them, and re-layouts  3.43 us
    another operation x2, other arithmetic, local_step(): jnp.stack([((clean + levels * noise) / root).astype(bf16), (clean * (2.0...  3.41 us

profile of v2, /device:TPU:0, one launch (start us, length us, event | category | flops | bytes accessed | tf_op | source)
XLA Modules:
  0.0 141.1 jit_solution(15751192132592733657)
XLA Ops:
  0.7 1.3 fusion.9
  5.9 1.4 reshape.39
  7.3 0.1 broadcast_in_dim.17
  7.4 0.6 broadcast_in_dim.18.refs_2_
  8.1 0.7 add_exponential_fusion
  8.8 0.1 broadcast_bitcast_fusion
  8.9 2.2 %fusion.1 = (bf16[1,336,1024]{2,1,0:T(8,128)(2,1)S(1)}, bf16[1,336,1024]{2,1,0:T(8,128)(2,1)S(1)}) fusion(f32[1024]{0:T(1024)S(1)} %get-tuple-element.10, f32[336,1024]{1,0:T(8,128)} %param.6, f32[336,1024]{1,0:T(8,128)} %param.7, f32[1024]{0:T(1024)S(1)} %bitcast.29, f32[1024]{0:T(1024)S(1)} %get-tuple-element.11, f32[1024]{0:T(1024)S(1)} %get-tuple-element.12), kind=kLoop, calls=%fused_computation.4 | loop fusion | flops 2752512 | bytes 4145152 | tf_op jit(solution)/shard_map/stack | solution.py:439
  11.1 0.0 copy-start
  11.1 0.0 copy-start.1
  11.1 1.2 pad_maximum_fusion.refs_1_
  12.3 0.0 copy-done
  12.4 0.0 copy-done.1
  12.4 0.7 fusion.7.refs_0_
  13.1 124.6 %shard_map.77 = (f32[168,336]{1,0:T(8,128)}, f32[168,336]{1,0:T(8,128)}) custom-call(bf16[2,176,384]{2,1,0:T(8,128)(2,1)} %fusion.7.refs_0_, bf16[2,336,1024]{2,1,0:T(8,128)(2,1)} %pad_maximum_fusion.refs_1_, f32[2,8,704]{2,1,0:T(8,128)} %broadcast_in_dim.18.refs_2_, f32[168,336]{1,0:T(8,128)} %bitcast.25, f32[168,336]{1,0:T(8,128)} %bitcast.24), custom_call_target="tpu_custom_call" | custom-call | tf_op jit(solution)/shard_map/pallas_call | solution.py:456
  137.7 1.7 %copy.15 = f32[1,336,168]{1,2,0:T(8,128)} copy(f32[1,336,168]{1,2,0:T(8,128)} %bitcast.27) | data formatting | bytes 451584
  139.4 1.7 %copy.16 = f32[1,168,336]{2,1,0:T(8,128)} copy(f32[1,168,336]{2,1,0:T(8,128)} %bitcast.26) | data formatting | bytes 451584
  (8 shorter events, 0.1 us)
Async XLA Ops:
  11.1 1.3 copy-start
  11.1 1.3 copy-start.1

commit v3 on v1

--- a/solution.py
+++ b/solution.py
@@ -227,21 +227,23 @@
     send(None, sto.at[0, :, pix(z)], st.at[core, chan(z)], (S_F, z), (R_F, z), dev_p)
     for d in range(1, rows + 1):
         if d < rows:
-            state_out(d)
             low, high = z - d, z + d
             arrive(low >= 0, blk(low, xy), (R_Z, low))
             spread(low >= 0, low, blk(low, xy), True, False)
             arrive(high < rows, blk(high, xy), (R_Z, high))
             spread(high < rows, high, blk(high, xy), False, True)
+        if d == rows - 2:
+            for k in range(1, rows):
+                state_out(k)
+        if d == rows - 1:
+            for k in range(1, rows):
+                zt = ring[k]
+                send(None, sto.at[1, :, pix(zt)], tg.at[chan(z)], (S_T, k), (R_T, z), (zt, col))
         if d == 1:
             diagonal(None, z)
         else:
             diagonal(z - (d - 1) >= 0, z - (d - 1))
             diagonal(z + (d - 1) < rows, z + (d - 1))
-        if d == rows - 1:
-            for k in range(1, rows):
-                zt = ring[k]
-                send(None, sto.at[1, :, pix(zt)], tg.at[chan(z)], (S_T, k), (R_T, z), (zt, col))
     for k in range(1, rows):
         zb = ring[rows - k]
         arrive(None, st.at[core, chan(zb)], (R_S, zb))

time: 128 us -> 122 us (0.953)
  the two profiles are of different devices: /device:TPU:11 before, /device:TPU:0 now
where the time goes in v3:
time: 122 us; the launch traced here: 121 us
  Pallas kernels  106 us (87%)
  other arithmetic  7.77 us (6%)
  local copies, waits for them, and re-layouts  6.38 us (5%)
    pallas_call x1, Pallas kernels, local_step(): pl.pallas_call(lambda *refs: step_kernel(hb, ib, samples, *refs), out_sha...  106 us
    unnamed x13, local copies, waits for them, and re-layouts  3.46 us
    another operation x2, other arithmetic, local_step(): jnp.stack([((clean + levels * noise) / root).astype(bf16), (clean * (2.0...  3.41 us

profile of v3, /device:TPU:0, one launch (start us, length us, event | category | flops | bytes accessed | tf_op | source)
XLA Modules:
  0.0 121.3 jit_solution(15192127045284654312)
XLA Ops:
  0.6 0.7 add_exponential_fusion
  1.4 0.1 broadcast_bitcast_fusion
  1.5 2.2 %fusion.1 = (bf16[1,336,1024]{2,1,0:T(8,128)(2,1)S(1)}, bf16[1,336,1024]{2,1,0:T(8,128)(2,1)S(1)}) fusion(f32[1024]{0:T(1024)S(1)} %get-tuple-element.8, f32[336,1024]{1,0:T(8,128)} %param.6, f32[336,1024]{1,0:T(8,128)} %param.7, f32[1024]{0:T(1024)S(1)} %bitcast.31, f32[1024]{0:T(1024)S(1)} %get-tuple-element.9, f32[1024]{0:T(1024)S(1)} %get-tuple-element.10), kind=kLoop, calls=%fused_computation.5 | loop fusion | flops 2752512 | bytes 4145152 | tf_op jit(solution)/shard_map/stack | solution.py:438
  3.7 0.0 copy-start.3
  3.7 0.0 copy-start.2
  3.7 1.2 %pad_maximum_fusion.refs_1_ = bf16[2,336,1024]{2,1,0:T(8,128)(2,1)} fusion(bf16[1,336,1024]{2,1,0:T(8,128)(2,1)S(1)} %get-tuple-element.7, bf16[1,336,1024]{2,1,0:T(8,128)(2,1)S(1)} %get-tuple-element.6), kind=kLoop, calls=%fused_computation.1 | loop fusion | flops 688128 | bytes 2752512 | tf_op jit(solution)/shard_map/stack | solution.py:438
  4.9 0.0 copy-start
  4.9 0.0 copy-start.1
  4.9 0.0 copy-done.3
  4.9 0.6 fusion.10
  5.5 1.4 %fusion.9 = s32[2]{0:T(128)S(1)} fusion(s32[1,1]{0,1:T(1,128)} %bitcast.6, s32[1,1]{0,1:T(1,128)} %bitcast.5), kind=kLoop, calls=%fused_computation.26 | loop fusion | flops 8 | bytes 16 | tf_op jit(solution)/shard_map/jit(_take)/jit(_where)/select_n | solution.py:446
  6.9 0.0 copy-done.2
  6.9 0.5 reshape_squeeze.3
  7.4 0.1 constant_dynamic-slice_fusion
  7.5 0.6 gather_fusion
  8.1 1.4 %compare_and_fusion = pred[2]{0:T(512)(128)(4,1)S(1)} fusion(s32[1]{0:T(128)} %get-tuple-element.12, s32[1]{0:T(128)} %get-tuple-element.11), kind=kLoop, calls=%fused_computation.25 | loop fusion | flops 14 | bytes 10 | tf_op jit(solution)/shard_map/jit(_take)/and | solution.py:446
  9.5 0.1 select_add_fusion
  9.6 1.2 reshape.139.refs_2_
  10.7 0.0 copy-done
  10.8 0.0 copy-done.1
  10.8 0.7 fusion.7.refs_0_
  11.5 106.4 %shard_map.77 = (f32[168,336]{1,0:T(8,128)}, f32[168,336]{1,0:T(8,128)}) custom-call(bf16[2,176,384]{2,1,0:T(8,128)(2,1)} %fusion.7.refs_0_, bf16[2,336,1024]{2,1,0:T(8,128)(2,1)} %pad_maximum_fusion.refs_1_, f32[2,704,1]{2,1,0:T(8,128)} %reshape.139.refs_2_, f32[168,336]{1,0:T(8,128)} %bitcast.26, f32[168,336]{1,0:T(8,128)} %bitcast.25), custom_call_target="tpu_custom_call" | custom-call | tf_op jit(solution)/shard_map/pallas_call | solution.py:451
  118.0 1.7 %copy.15 = f32[1,336,168]{1,2,0:T(8,128)} copy(f32[1,336,168]{1,2,0:T(8,128)} %bitcast.28) | data formatting | bytes 451584
  119.6 1.7 %copy.16 = f32[1,168,336]{2,1,0:T(8,128)} copy(f32[1,168,336]{2,1,0:T(8,128)} %bitcast.27) | data formatting | bytes 451584
  (7 shorter events, 0.1 us)
Async XLA Ops:
  3.7 1.3 %copy-start.3 = (s32[32]{0:T(128)S(1)}, s32[32]{0:T(128)}, u32[]{:S(2)}) copy-start(s32[32]{0:T(128)} %param.8) | copy-start | bytes 388
  3.7 3.2 %copy-start.2 = (f32[1,32,1344]{2,1,0:T(8,128)S(1)}, f32[1,32,1344]{2,1,0:T(8,128)}, u32[]{:S(2)}) copy-start(f32[1,32,1344]{2,1,0:T(8,128)} %param.9) | copy-start | bytes 516100
  4.9 5.8 %copy-start = (f32[1,168,336]{2,1,0:T(8,128)S(1)}, f32[1,168,336]{2,1,0:T(8,128)}, u32[]{:S(2)}) copy-start(f32[1,168,336]{2,1,0:T(8,128)} %param.11) | copy-start | bytes 677380
  4.9 5.8 %copy-start.1 = (f32[1,336,168]{1,2,0:T(8,128)S(1)}, f32[1,336,168]{1,2,0:T(8,128)}, u32[]{:S(2)}) copy-start(f32[1,336,168]{1,2,0:T(8,128)} %param.10) | copy-start | bytes 677380
